TPU v7x, 8 devices: a whole 2x2x1 slice. The times are simulated.
8 devices in a mesh: stage: 1 (over z), model: 2 (over y), data: 4 (over x, core).
Axes of the slice: x: 2, y: 2, z: 1, core: 2. Of those that a mesh axis runs over, the one named last changes fastest.
Arguments:
- w_fc1: float32 [32, 1536, 1024], P('stage', 'data', 'model')
- m_fc1: float32 [32, 1536, 1024], P('stage', 'data', 'model')
- g_fc1: bfloat16 [32, 1536, 1024], P('stage', 'data', 'model')
- w_fc2: float32 [32, 1536, 512], P('stage', 'data', 'model')
- m_fc2: float32 [32, 1536, 512], P('stage', 'data', 'model')
- g_fc2: bfloat16 [32, 1536, 512], P('stage', 'data', 'model')
Outputs:
- output 1: float32 [32, 1536, 1024], P('stage', 'data', 'model')
- output 2: float32 [32, 1536, 1024], P('stage', 'data', 'model')
- output 3: float32 [32, 1536, 512], P('stage', 'data', 'model')
- output 4: float32 [32, 1536, 512], P('stage', 'data', 'model')
All inputs are finite; a program needn't handle non-finite values.
Results may differ from a plain program's by a relative error of at most 0.00830859.
Values are sent between devices in bfloat16 or wider.
A program may use at most 1 GiB of HBM per device.

v0:
```python
import math
import jax
import jax.numpy as jnp
from jax import lax
from jax.sharding import PartitionSpec as P

NS_STEPS = 5
NS_COEF_A = 3.4445
NS_COEF_B = -4.7750
NS_COEF_C = 2.0315
MOMENTUM = 0.95
LEARN_RATE = 0.04
DECAY = 0.2
NORM_EPS = 1e-7


def newton_schulz(x_mat):
    row_count, col_count = x_mat.shape[1], x_mat.shape[2]
    for ns_step in range(NS_STEPS):
        if row_count <= col_count:
            gram_mat = jnp.einsum('emk,enk->emn', x_mat, x_mat, preferred_element_type=jnp.float32).astype(jnp.bfloat16)
        else:
            gram_mat = jnp.einsum('ekm,ekn->emn', x_mat, x_mat, preferred_element_type=jnp.float32).astype(jnp.bfloat16)
        gram_sq = jnp.einsum('emk,ekn->emn', gram_mat, gram_mat, preferred_element_type=jnp.float32)
        poly_mat = (NS_COEF_B * gram_mat.astype(jnp.float32) + NS_COEF_C * gram_sq).astype(jnp.bfloat16)
        if row_count <= col_count:
            update_term = jnp.einsum('emk,ekn->emn', poly_mat, x_mat, preferred_element_type=jnp.float32)
        else:
            update_term = jnp.einsum('emk,ekn->emn', x_mat, poly_mat, preferred_element_type=jnp.float32)
        x_mat = (NS_COEF_A * x_mat.astype(jnp.float32) + update_term).astype(jnp.bfloat16)
    return x_mat


def update_stack(w_loc, m_loc, g_loc, data_size, model_size):
    new_mom = MOMENTUM * m_loc + g_loc.astype(jnp.float32)
    mat_norms = jnp.sqrt(lax.psum(jnp.sum(new_mom * new_mom, axis=(1, 2)), ('data', 'model')))
    expert_count, rows_loc, cols_loc = m_loc.shape
    own_count = expert_count // data_size
    rows_full = rows_loc * data_size
    cols_full = cols_loc * model_size
    row_whole = lax.all_to_all(new_mom.astype(jnp.bfloat16), 'data', 0, 1, tiled=True)
    mom_whole = lax.all_gather(row_whole, 'model', axis=2, tiled=True)
    own_norms = lax.dynamic_slice_in_dim(mat_norms, lax.axis_index('data') * own_count, own_count)
    x_mat = (mom_whole.astype(jnp.float32) / (own_norms[:, None, None] + NORM_EPS)).astype(jnp.bfloat16)
    x_mat = newton_schulz(x_mat)
    x_cols = lax.dynamic_slice_in_dim(x_mat, lax.axis_index('model') * cols_loc, cols_loc, axis=2)
    x_back = lax.all_to_all(x_cols, 'data', 1, 0, tiled=True)
    step_scale = 0.2 * math.sqrt(max(rows_full, cols_full))
    new_w = w_loc - LEARN_RATE * (x_back.astype(jnp.float32) * step_scale + DECAY * w_loc)
    return new_w, new_mom


def solution(mesh):
    data_size = mesh.shape['data']
    model_size = mesh.shape['model']
    block_spec = P('stage', 'data', 'model')

    def local_step(w_fc1, m_fc1, g_fc1, w_fc2, m_fc2, g_fc2):
        new_w1, new_m1 = update_stack(w_fc1, m_fc1, g_fc1, data_size, model_size)
        new_w2, new_m2 = update_stack(w_fc2, m_fc2, g_fc2, data_size, model_size)
        return new_w1, new_m1, new_w2, new_m2

    return jax.shard_map(local_step, mesh=mesh, in_specs=(block_spec,) * 6, out_specs=(block_spec,) * 4, check_vma=False)
```

profile of v0, /device:TPU:0, one launch (start us, length us, event | category | flops | bytes accessed | tf_op | source)
XLA Modules:
  0.0 1339.8 jit_solution(3172307350001191785)
XLA Ops:
  19.9 75.0 %all_to_all.54 = bf16[32,384,256]{2,1,0:T(8,128)(2,1)S(1)} all-to-all(bf16[32,384,256]{2,1,0:T(8,128)(2,1)S(1)} %get-tuple-element.6), channel_id=1, replica_groups=mesh['stage'=1,'model'=2,'data'=4] {'data'}, dimensions={0} | all-to-all | bytes 12582912 | tf_op jit(solution)/shard_map/all_to_all | solution.py:41
  98.0 14.9 %multiply_reduce_fusion = (f32[32]{0:T(128)S(1)}, f32[32,384,512]{2,1,0:T(8,128)S(1)}) fusion(bf16[32,384,512]{2,1,0:T(8,128)(2,1)} %param.8, f32[32,384,512]{2,1,0:T(8,128)} %param.7), kind=kLoop, calls=%fused_computation.21 | loop fusion | flops 31457248 | bytes 62914688 | tf_op jit(solution)/shard_map/reduce_sum | solution.py:36
  139.3 149.9 %all-reduce = (f32[32]{0:T(128)S(1)}, f32[32]{0:T(128)S(1)}) all-reduce(f32[32]{0:T(128)S(1)} %get-tuple-element.8, f32[32]{0:T(128)S(1)} %multiply_reduce_fusion.1), channel_id=1, replica_groups=mesh['stage'=1,'model'=2,'data'=4] {'data','model'}, use_global_device_ids=true, to_apply=%region_1.0 | all-reduce | flops 64 | bytes 512 | tf_op jit(solution)/shard_map/psum | solution.py:36
  300.6 17.1 %convolution_convert_fusion.9 = bf16[8,512,512]{2,1,0:T(8,128)(2,1)} fusion(bf16[8,1536,512]{2,1,0:T(8,128)(2,1)} %all-gather.5.cloned.1.call-done, f32[8]{0:T(128)S(1)} %dynamic-slice_add_fusion.2), kind=kOutput, calls=%fused_computation.67 | convolution fusion | flops 6463422464 | bytes 16777248 | tf_op jit(solution)/shard_map/ekm,ekn->emn/dot_general | solution.py:23
  317.6 24.8 %add_convert_fusion.12 = bf16[8,1536,512]{2,1,0:T(8,128)(2,1)} fusion(bf16[8,512,512]{2,1,0:T(8,128)(2,1)} %convolution_convert_fusion.9, f32[8]{0:T(128)S(1)} %dynamic-slice_add_fusion.2, bf16[8,1536,512]{2,1,0:T(8,128)(2,1)} %all-gather.5.cloned.1.call-done), kind=kOutput, calls=%fused_computation.18 | convolution fusion | flops 8663334912 | bytes 29360160 | tf_op jit(solution)/shard_map/emk,ekn->emn/dot_general | solution.py:29
  342.5 14.7 %convolution_convert_fusion.8 = bf16[8,512,512]{2,1,0:T(8,128)(2,1)} fusion(bf16[8,1536,512]{2,1,0:T(8,128)(2,1)} %add_convert_fusion.12), kind=kOutput, calls=%fused_computation.66 | convolution fusion | flops 6444548096 | bytes 16777216 | tf_op jit(solution)/shard_map/ekm,ekn->emn/dot_general | solution.py:23
  357.2 27.2 %add_convert_fusion.11 = bf16[8,1536,512]{2,1,0:T(8,128)(2,1)} fusion(bf16[8,1536,512]{2,1,0:T(8,128)(2,1)} %add_convert_fusion.12, bf16[8,512,512]{2,1,0:T(8,128)(2,1)} %convolution_convert_fusion.8), kind=kOutput, calls=%fused_computation.17 | convolution fusion | flops 8625586176 | bytes 29360128 | tf_op jit(solution)/shard_map/emk,ekn->emn/dot_general | solution.py:29
  384.4 14.7 %convolution_convert_fusion.7 = bf16[8,512,512]{2,1,0:T(8,128)(2,1)} fusion(bf16[8,1536,512]{2,1,0:T(8,128)(2,1)} %add_convert_fusion.11), kind=kOutput, calls=%fused_computation.65 | convolution fusion | flops 6444548096 | bytes 16777216 | tf_op jit(solution)/shard_map/ekm,ekn->emn/dot_general | solution.py:23
  399.1 27.3 %add_convert_fusion.10 = bf16[8,1536,512]{2,1,0:T(8,128)(2,1)} fusion(bf16[8,1536,512]{2,1,0:T(8,128)(2,1)} %add_convert_fusion.11, bf16[8,512,512]{2,1,0:T(8,128)(2,1)} %convolution_convert_fusion.7), kind=kOutput, calls=%fused_computation.16 | convolution fusion | flops 8625586176 | bytes 29360128 | tf_op jit(solution)/shard_map/emk,ekn->emn/dot_general | solution.py:29
  426.4 14.7 %convolution_convert_fusion.6 = bf16[8,512,512]{2,1,0:T(8,128)(2,1)} fusion(bf16[8,1536,512]{2,1,0:T(8,128)(2,1)} %add_convert_fusion.10), kind=kOutput, calls=%fused_computation.64 | convolution fusion | flops 6444548096 | bytes 16777216 | tf_op jit(solution)/shard_map/ekm,ekn->emn/dot_general | solution.py:23
  441.1 27.3 %add_convert_fusion.9 = bf16[8,1536,512]{2,1,0:T(8,128)(2,1)} fusion(bf16[8,1536,512]{2,1,0:T(8,128)(2,1)} %add_convert_fusion.10, bf16[8,512,512]{2,1,0:T(8,128)(2,1)} %convolution_convert_fusion.6), kind=kOutput, calls=%fused_computation.15 | convolution fusion | flops 8625586176 | bytes 29360128 | tf_op jit(solution)/shard_map/emk,ekn->emn/dot_general | solution.py:29
  468.4 14.7 %convolution_convert_fusion.5 = bf16[8,512,512]{2,1,0:T(8,128)(2,1)} fusion(bf16[8,1536,512]{2,1,0:T(8,128)(2,1)} %add_convert_fusion.9), kind=kOutput, calls=%fused_computation.63 | convolution fusion | flops 6444548096 | bytes 16777216 | tf_op jit(solution)/shard_map/ekm,ekn->emn/dot_general | solution.py:23
  483.1 22.8 %fusion.17 = f32[8,1536,512]{2,1,0:T(8,128)} fusion(bf16[8,1536,512]{2,1,0:T(8,128)(2,1)} %add_convert_fusion.9, bf16[8,512,512]{2,1,0:T(8,128)(2,1)} %convolution_convert_fusion.5), kind=kOutput, calls=%fused_computation.52 | convolution fusion | flops 8600420352 | bytes 41943040 | tf_op jit(solution)/shard_map/emk,ekn->emn/dot_general | solution.py:29
  530.1 62.5 %all-gather.3.cloned.1.call-done = bf16[8,1536,1024]{2,1,0:T(8,128)(2,1)} async-done(((bf16[8,1536,512]{2,1,0:T(8,128)(2,1)}), bf16[8,1536,1024]{2,1,0:T(8,128)(2,1)}) %all-gather.3.cloned.1.call-update) | async-done | bytes 25165840 | tf_op jit(solution)/shard_map/all_gather | solution.py:42
  592.6 40.5 %convolution_convert_fusion.4 = bf16[8,1024,1024]{2,1,0:T(8,128)(2,1)} fusion(bf16[8,1536,1024]{2,1,0:T(8,128)(2,1)} %all-gather.3.cloned.1.call-done, f32[8]{0:T(128)S(1)} %copy-done.1), kind=kOutput, calls=%fused_computation.46 | convolution fusion | flops 25815941120 | bytes 41943072 | tf_op jit(solution)/shard_map/ekm,ekn->emn/dot_general | solution.py:23
  633.1 30.6 %add_convert_fusion.35 = bf16[8,1024,1024]{2,1,0:T(8,128)(2,1)} fusion(bf16[8,1024,1024]{2,1,0:T(8,128)(2,1)} %convolution_convert_fusion.4), kind=kOutput, calls=%fused_computation.9.clone.clone.2 | convolution fusion | flops 17221812224 | bytes 33554432 | tf_op jit(solution)/shard_map/emk,ekn->emn/dot_general | solution.py:24
  663.6 39.9 %add_convert_fusion.3 = bf16[8,1536,1024]{2,1,0:T(8,128)(2,1)} fusion(f32[8]{0:T(128)S(1)} %copy-done.1, bf16[8,1536,1024]{2,1,0:T(8,128)(2,1)} %all-gather.3.cloned.1.call-done, bf16[8,1024,1024]{2,1,0:T(8,128)(2,1)} %add_convert_fusion.35), kind=kOutput, calls=%fused_computation.3 | convolution fusion | flops 25895632896 | bytes 67108896 | tf_op jit(solution)/shard_map/emk,ekn->emn/dot_general | solution.py:29
  703.5 37.2 %convolution_convert_fusion.3 = bf16[8,1024,1024]{2,1,0:T(8,128)(2,1)} fusion(bf16[8,1536,1024]{2,1,0:T(8,128)(2,1)} %add_convert_fusion.3), kind=kOutput, calls=%fused_computation.45 | convolution fusion | flops 25778192384 | bytes 41943040 | tf_op jit(solution)/shard_map/ekm,ekn->emn/dot_general | solution.py:23
  740.7 58.1 %add_convert_fusion.2 = bf16[8,1536,1024]{2,1,0:T(8,128)(2,1)} fusion(bf16[8,1536,1024]{2,1,0:T(8,128)(2,1)} %add_convert_fusion.3, bf16[8,1024,1024]{2,1,0:T(8,128)(2,1)} %convolution_convert_fusion.3), kind=kOutput, calls=%fused_computation.2 | convolution fusion | flops 43041947648 | bytes 67108864 | tf_op jit(solution)/shard_map/emk,ekn->emn/dot_general | solution.py:29
  798.8 37.0 %convolution_convert_fusion.2 = bf16[8,1024,1024]{2,1,0:T(8,128)(2,1)} fusion(bf16[8,1536,1024]{2,1,0:T(8,128)(2,1)} %add_convert_fusion.2), kind=kOutput, calls=%fused_computation.44 | convolution fusion | flops 25778192384 | bytes 41943040 | tf_op jit(solution)/shard_map/ekm,ekn->emn/dot_general | solution.py:23
  835.8 57.7 %add_convert_fusion.1 = bf16[8,1536,1024]{2,1,0:T(8,128)(2,1)} fusion(bf16[8,1536,1024]{2,1,0:T(8,128)(2,1)} %add_convert_fusion.2, bf16[8,1024,1024]{2,1,0:T(8,128)(2,1)} %convolution_convert_fusion.2), kind=kOutput, calls=%fused_computation.1 | convolution fusion | flops 43041947648 | bytes 67108864 | tf_op jit(solution)/shard_map/emk,ekn->emn/dot_general | solution.py:29
  893.5 37.2 %convolution_convert_fusion.1 = bf16[8,1024,1024]{2,1,0:T(8,128)(2,1)} fusion(bf16[8,1536,1024]{2,1,0:T(8,128)(2,1)} %add_convert_fusion.1), kind=kOutput, calls=%fused_computation.43 | convolution fusion | flops 25778192384 | bytes 41943040 | tf_op jit(solution)/shard_map/ekm,ekn->emn/dot_general | solution.py:23
  930.7 57.5 %add_convert_fusion = bf16[8,1536,1024]{2,1,0:T(8,128)(2,1)} fusion(bf16[8,1536,1024]{2,1,0:T(8,128)(2,1)} %add_convert_fusion.1, bf16[8,1024,1024]{2,1,0:T(8,128)(2,1)} %convolution_convert_fusion.1), kind=kOutput, calls=%fused_computation | convolution fusion | flops 43041947648 | bytes 67108864 | tf_op jit(solution)/shard_map/emk,ekn->emn/dot_general | solution.py:29
  988.2 37.2 %convolution_convert_fusion = bf16[8,1024,1024]{2,1,0:T(8,128)(2,1)} fusion(bf16[8,1536,1024]{2,1,0:T(8,128)(2,1)} %add_convert_fusion), kind=kOutput, calls=%fused_computation.42 | convolution fusion | flops 25778192384 | bytes 41943040 | tf_op jit(solution)/shard_map/ekm,ekn->emn/dot_general | solution.py:23
  1025.4 31.1 %add_convert_fusion.36 = bf16[8,1024,1024]{2,1,0:T(8,128)(2,1)} fusion(bf16[8,1024,1024]{2,1,0:T(8,128)(2,1)} %convolution_convert_fusion), kind=kOutput, calls=%fused_computation.5.clone.clone.1 | convolution fusion | flops 17221812224 | bytes 33554432 | tf_op jit(solution)/shard_map/emk,ekn->emn/dot_general | solution.py:24
  1056.5 39.8 %fusion.3 = f32[8,1536,1024]{2,1,0:T(8,128)} fusion(bf16[8,1536,1024]{2,1,0:T(8,128)(2,1)} %add_convert_fusion, bf16[8,1024,1024]{2,1,0:T(8,128)(2,1)} %add_convert_fusion.36), kind=kOutput, calls=%fused_computation.23 | convolution fusion | flops 25769803776 | bytes 92274688 | tf_op jit(solution)/shard_map/emk,ekn->emn/dot_general | solution.py:29
  1096.3 13.2 fusion
  1109.5 30.0 %copy.30 = bf16[8,1536,512]{2,0,1:T(8,128)(2,1)} copy(bf16[8,1536,512]{2,1,0:T(8,128)(2,1)S(1)} %fusion) | data formatting | bytes 25165824 | tf_op jit(solution)/shard_map/dynamic_slice | solution.py:46
  1166.3 14.6 %fusion.16 = f32[32,384,256]{2,1,0:T(8,128)} fusion(f32[32,384,256]{2,1,0:T(8,128)} %param.9, f32[4,8,384,256]{3,2,1,0:T(8,128)} %copy.39), kind=kLoop, calls=%fused_computation.38 | loop fusion | flops 12582912 | bytes 37748736 | tf_op jit(solution)/shard_map/sub | solution.py:49
  1180.9 102.7 %all-to-all-done.1 = bf16[8,1536,512]{2,0,1:T(8,128)(2,1)} async-done(((bf16[8,1536,512]{2,0,1:T(8,128)(2,1)}), bf16[8,1536,512]{2,0,1:T(8,128)(2,1)}, u32[]{:S(2)}, u32[]{:S(2)}) %all-to-all-start.1) | async-done | bytes 12582944 | tf_op jit(solution)/shard_map/all_to_all | solution.py:47
  1291.1 16.7 %copy.31 = f32[4,8,384,512]{3,2,1,0:T(8,128)} copy(f32[4,8,384,512]{3,1,2,0:T(8,128)S(1)} %bitcast.92) | data formatting | bytes 50331648 | tf_op jit(solution)/shard_map/mul | solution.py:49
  1307.8 25.0 %fusion.2 = f32[32,384,512]{2,1,0:T(8,128)} fusion(f32[32,384,512]{2,1,0:T(8,128)} %param.6, f32[4,8,384,512]{3,2,1,0:T(8,128)} %copy.31), kind=kLoop, calls=%fused_computation.14 | loop fusion | flops 25165824 | bytes 75497472 | tf_op jit(solution)/shard_map/sub | solution.py:49
  (28 shorter events, 112.1 us)
Async XLA Ops:
  7.2 293.4 %all-gather.5.cloned.1.call-start = ((), (), s32[]{:S(2)}) async-start(), calls=%async_computation.5 | async-start | bytes 18874368 | tf_op jit(solution)/shard_map/all_gather | solution.py:42
  112.9 8.9 copy-start
  127.3 162.6 %all-to-all-start = ((bf16[32,384,512]{2,1,0:T(8,128)(2,1)}), bf16[32,384,512]{2,1,0:T(8,128)(2,1)}, u32[]{:S(2)}, u32[]{:S(2)}) async-start(bf16[32,384,512]{2,1,0:T(8,128)(2,1)} %convert_element_type.187), calls=%async_computation | async-start | bytes 25165824 | tf_op jit(solution)/shard_map/all_to_all | solution.py:41
  133.7 458.9 %all-gather.3.cloned.1.call-start = ((), (), s32[]{:S(2)}) async-start(), calls=%async_computation.4 | async-start | bytes 37748736 | tf_op jit(solution)/shard_map/all_gather | solution.py:42
  516.6 76.0 %copy-start.1 = (f32[8]{0:T(128)S(1)}, f32[8]{0:T(128)}, u32[]{:S(2)}) copy-start(f32[8]{0:T(128)} %dynamic-slice_add_fusion.3) | copy-start | bytes 100
  524.7 614.8 %all-to-all-start.3 = ((bf16[8,1536,256]{2,0,1:T(8,128)(2,1)}), bf16[8,1536,256]{2,0,1:T(8,128)(2,1)}, u32[]{:S(2)}, u32[]{:S(2)}) async-start(bf16[8,1536,256]{2,0,1:T(8,128)(2,1)} %copy.38), calls=%async_computation.3 | async-start | bytes 12582912 | tf_op jit(solution)/shard_map/all_to_all | solution.py:47
  1139.5 144.1 %all-to-all-start.1 = ((bf16[8,1536,512]{2,0,1:T(8,128)(2,1)}), bf16[8,1536,512]{2,0,1:T(8,128)(2,1)}, u32[]{:S(2)}, u32[]{:S(2)}) async-start(bf16[8,1536,512]{2,0,1:T(8,128)(2,1)} %copy.30), calls=%async_computation.1 | async-start | bytes 25165824 | tf_op jit(solution)/shard_map/all_to_all | solution.py:47
Sparse Core Ops, SparseCore 0:
  98.1 151.0 all-gather.4
  300.6 291.8 all-gather.2
where the time goes:
time: 1340 us
  matrix products  709 us (53%)
  blocking collectives  225 us (17%)
  waiting for transfers between devices  165 us (12%)
  other arithmetic  118 us (9%)
  local copies, waits for them, and re-layouts  90.3 us (7%)
  starting transfers between devices  18.1 us (1%)
  between operations  14.3 us (1%)
    dot_general x10, matrix products, newton_schulz(): jnp.einsum('emk,ekn->emn', x_mat, poly_mat, preferred_element_type=jnp.fl...  382 us
    dot_general x10, matrix products, newton_schulz(): jnp.einsum('ekm,ekn->emn', x_mat, x_mat, preferred_element_type=jnp.float32)  265 us
    psum x1, blocking collectives, update_stack(): lax.psum(jnp.sum(new_mom * new_mom, axis=(1, 2)), ('data', 'model'))  150 us
    all_to_all x2, waiting for transfers between devices, update_stack(): x_back = lax.all_to_all(x_cols, 'data', 1, 0, tiled=True)  103 us
    all_to_all x1, blocking collectives, update_stack(): lax.all_to_all(new_mom.astype(jnp.bfloat16), 'data', 0, 1, tiled=True)  75 us
    all_gather x2, waiting for transfers between devices, update_stack(): mom_whole = lax.all_gather(row_whole, 'model', axis=2, tiled=True)  62.5 us
    dot_general x2, matrix products, newton_schulz(): jnp.einsum('emk,ekn->emn', gram_mat, gram_mat, preferred_element_type=jnp...  61.7 us
    sub x2, other arithmetic, update_stack(): w_loc - LEARN_RATE * (x_back.astype(jnp.float32) * step_scale + DECAY * w...  39.6 us
  transfers between devices with their start and end apart: 5, of which 2 were waited for; matrix products, arithmetic and copies ran while one was open for 63% of the time, Pallas kernels for 0%

commit v1 on v0

v1 whole, which is shorter than its diff:
```python
import functools
import math
import jax
import jax.numpy as jnp
from jax import lax
from jax.experimental import pallas as pl
from jax.experimental.pallas import tpu as pltpu
from jax.sharding import PartitionSpec as P

NS_STEPS = 5
NS_COEF_A = 3.4445
NS_COEF_B = -4.7750
NS_COEF_C = 2.0315
MOMENTUM = 0.95
LEARN_RATE = 0.04
DECAY = 0.2
NORM_EPS = 1e-7

MESH_ID = pl.DeviceIdType.MESH
GRAM_BLOCK = 256
ROW_BLOCK = 512


def momentum_kernel(m_ref, g_ref, new_m_ref, low_ref, sq_ref):
    new_mom = MOMENTUM * m_ref[0] + g_ref[0].astype(jnp.float32)
    new_m_ref[0] = new_mom
    low_ref[0] = new_mom.astype(jnp.bfloat16)
    squares = new_mom * new_mom
    rows, cols = squares.shape
    part = jnp.sum(squares.reshape(rows // 8, 8, cols), axis=0)
    total = part[:, :128]
    for start in range(128, cols, 128):
        total = total + part[:, start:start + 128]
    sq_ref[0, 0] = total


def momentum_step(m_loc, g_loc, owners):
    experts, rows, cols = m_loc.shape
    rounds = experts // owners
    block = pl.BlockSpec((1, rows, cols), lambda e: (e, 0, 0))
    return pl.pallas_call(
        momentum_kernel,
        grid=(experts,),
        in_specs=[block, block],
        out_specs=[block, block, pl.BlockSpec((1, 1, 8, 128), lambda e: (e % owners, e // owners, 0, 0))],
        out_shape=[
            jax.ShapeDtypeStruct(m_loc.shape, jnp.float32),
            jax.ShapeDtypeStruct(m_loc.shape, jnp.bfloat16),
            jax.ShapeDtypeStruct((owners, rounds, 8, 128), jnp.float32),
        ],
        compiler_params=pltpu.CompilerParams(dimension_semantics=('arbitrary',), vmem_limit_bytes=32 * 2 ** 20),
        name='momentum',
    )(m_loc, g_loc)


def iterate(x_ref, gram_ref, poly_ref):
    rows, cols = x_ref.shape
    gram_block = min(GRAM_BLOCK, cols)
    row_block = min(ROW_BLOCK, rows)

    @pl.loop(0, NS_STEPS)
    def ns_step(_):
        @pl.loop(0, cols // gram_block)
        def gram(i):
            span = pl.ds(pl.multiple_of(i * gram_block, gram_block), gram_block)
            part = lax.dot_general(x_ref[:, span], x_ref[...], (((0,), (0,)), ((), ())), preferred_element_type=jnp.float32)
            gram_ref[span, :] = part.astype(jnp.bfloat16)

        @pl.loop(0, cols // gram_block)
        def poly(i):
            span = pl.ds(pl.multiple_of(i * gram_block, gram_block), gram_block)
            gram_rows = gram_ref[span, :]
            gram_sq = jnp.dot(gram_rows, gram_ref[...], preferred_element_type=jnp.float32)
            poly_ref[span, :] = (NS_COEF_B * gram_rows.astype(jnp.float32) + NS_COEF_C * gram_sq).astype(jnp.bfloat16)

        @pl.loop(0, rows // row_block)
        def update(i):
            span = pl.ds(pl.multiple_of(i * row_block, row_block), row_block)
            x_rows = x_ref[span, :]
            term = jnp.dot(x_rows, poly_ref[...], preferred_element_type=jnp.float32)
            x_ref[span, :] = (NS_COEF_A * x_rows.astype(jnp.float32) + term).astype(jnp.bfloat16)


def exchange_kernel(low1, low2, sq1, sq2, back1, back2, x1, x2, sums1, sums2, gram1, poly1, gram2, poly2,
                    fwd1, fwd2, got1, got2, ret1, ret2, done_sems, sq_send, sq_got):
    model = lax.axis_index('model')
    data = lax.axis_index('data')
    chip, core = data // 2, data % 2
    me = model * 4 + data
    owners = 8
    rounds = low1.shape[0] // owners

    offsets = [(1, 0, 0), (0, 1, 0), (1, 0, 1), (0, 1, 1), (1, 1, 0), (1, 1, 1), (0, 0, 1)]
    others = [((model + dm) % 2, ((chip + dx) % 2) * 2 + (core + dc) % 2) for dm, dx, dc in offsets]

    barrier = pltpu.get_barrier_semaphore()
    for peer_model, peer_data in others:
        pl.semaphore_signal(barrier, inc=1, device_id=(0, peer_model, peer_data), device_id_type=MESH_ID)
    pl.semaphore_wait(barrier, len(others))

    def window(x_ref, k, at_model, at_data):
        rows, cols = x_ref.shape[1] // 4, x_ref.shape[2] // 2
        return x_ref.at[k, pl.ds(pl.multiple_of(at_data * rows, rows), rows), pl.ds(pl.multiple_of(at_model * cols, cols), cols)]

    for src, dst, t in ((sq2, sums2, 0), (sq1, sums1, 1)):
        for peer_model, peer_data in others:
            pltpu.make_async_remote_copy(src.at[peer_model * 4 + peer_data], dst.at[me], sq_send.at[t], sq_got.at[t],
                                         device_id=(0, peer_model, peer_data), device_id_type=MESH_ID).start()
        pltpu.make_async_copy(src.at[me], dst.at[me], sq_got.at[t]).start()

    def send_round(k):
        for src, x_ref, sems, got in ((low2, x2, fwd2, got2), (low1, x1, fwd1, got1)):
            for peer_model, peer_data in others:
                pltpu.make_async_remote_copy(src.at[k * owners + peer_model * 4 + peer_data], window(x_ref, k, model, data),
                                             sems.at[k], got.at[k],
                                             device_id=(0, peer_model, peer_data), device_id_type=MESH_ID).start()
            pltpu.make_async_copy(src.at[k * owners + me], window(x_ref, k, model, data), got.at[k]).start()

    def return_round(k, x_ref, dst, sems, t):
        for peer_model, peer_data in others:
            pltpu.make_async_remote_copy(window(x_ref, k, peer_model, peer_data), dst.at[k * owners + me],
                                         sems.at[k], done_sems.at[t],
                                         device_id=(0, peer_model, peer_data), device_id_type=MESH_ID).start()
        pltpu.make_async_copy(window(x_ref, k, model, data), dst.at[k * owners + me], done_sems.at[t]).start()

    def wait_bytes(ref, sem):
        pltpu.make_async_copy(ref, ref, sem).wait()

    def orthogonalize(k, x_ref, sums_ref, gram_ref, poly_ref):
        norm = jnp.sqrt(jnp.sum(sums_ref[:, k])) + NORM_EPS
        rows = x_ref.shape[1]

        @pl.loop(0, rows // 256)
        def normalize(i):
            span = pl.ds(pl.multiple_of(i * 256, 256), 256)
            x_ref[k, span, :] = (x_ref[k, span, :].astype(jnp.float32) / norm).astype(jnp.bfloat16)

        iterate(x_ref.at[k], gram_ref, poly_ref)

    @pl.loop(0, rounds)
    def forward(k):
        send_round(k)

    wait_bytes(sums2, sq_got.at[0])
    wait_bytes(sums1, sq_got.at[1])

    @pl.loop(0, rounds)
    def work(k):
        wait_bytes(x2.at[k], got2.at[k])
        orthogonalize(k, x2, sums2, gram2, poly2)
        return_round(k, x2, back2, ret2, 0)
        wait_bytes(x1.at[k], got1.at[k])
        orthogonalize(k, x1, sums1, gram1, poly1)
        return_round(k, x1, back1, ret1, 1)

    for src, t in ((sq2, 0), (sq1, 1)):
        wait_bytes(src.at[pl.ds(0, len(others))], sq_send.at[t])

    @pl.loop(0, rounds)
    def finish(k):
        for low, fwd, ret in ((low2, fwd2, ret2), (low1, fwd1, ret1)):
            sent = low.at[pl.ds(0, len(others))]
            wait_bytes(sent, fwd.at[k])
            wait_bytes(sent, ret.at[k])

    wait_bytes(back2, done_sems.at[0])
    wait_bytes(back1, done_sems.at[1])


def exchange(low1, low2, sq1, sq2):
    owners, rounds = sq1.shape[:2]
    _, rows1, cols1 = low1.shape
    _, rows2, cols2 = low2.shape
    any_spec = pl.BlockSpec(memory_space=pl.ANY)
    flops = 2 * rounds * NS_STEPS * sum(2 * 4 * r * (2 * c) ** 2 + (2 * c) ** 3 for r, c in ((rows1, cols1), (rows2, cols2)))
    dma = pltpu.SemaphoreType.DMA
    return pl.pallas_call(
        exchange_kernel,
        in_specs=[any_spec] * 4,
        out_specs=[any_spec] * 2,
        out_shape=[jax.ShapeDtypeStruct(low1.shape, low1.dtype), jax.ShapeDtypeStruct(low2.shape, low2.dtype)],
        scratch_shapes=[
            pltpu.VMEM((rounds, 4 * rows1, 2 * cols1), jnp.bfloat16),
            pltpu.VMEM((rounds, 4 * rows2, 2 * cols2), jnp.bfloat16),
            pltpu.VMEM((owners, rounds, 8, 128), jnp.float32),
            pltpu.VMEM((owners, rounds, 8, 128), jnp.float32),
            pltpu.VMEM((2 * cols1, 2 * cols1), jnp.bfloat16),
            pltpu.VMEM((2 * cols1, 2 * cols1), jnp.bfloat16),
            pltpu.VMEM((2 * cols2, 2 * cols2), jnp.bfloat16),
            pltpu.VMEM((2 * cols2, 2 * cols2), jnp.bfloat16),
            dma((rounds,)), dma((rounds,)), dma((rounds,)), dma((rounds,)), dma((rounds,)), dma((rounds,)),
            dma((2,)), dma((2,)), dma((2,)),
        ],
        compiler_params=pltpu.CompilerParams(collective_id=0, has_side_effects=True, vmem_limit_bytes=56 * 2 ** 20),
        cost_estimate=pl.CostEstimate(flops=flops, bytes_accessed=4 * (low1.size + low2.size), transcendentals=0),
        name='exchange',
    )(low1, low2, sq1, sq2)


def weight_step(w_loc, x_back, rows_full, cols_full):
    step_scale = 0.2 * math.sqrt(max(rows_full, cols_full))
    return w_loc - LEARN_RATE * (x_back.astype(jnp.float32) * step_scale + DECAY * w_loc)


def solution(mesh):
    data_size = mesh.shape['data']
    model_size = mesh.shape['model']
    owners = data_size * model_size
    block_spec = P('stage', 'data', 'model')

    def local_step(w_fc1, m_fc1, g_fc1, w_fc2, m_fc2, g_fc2):
        new_m2, low2, sq2 = momentum_step(m_fc2, g_fc2, owners)
        new_m1, low1, sq1 = momentum_step(m_fc1, g_fc1, owners)
        back1, back2 = exchange(low1, low2, sq1, sq2)
        full = [(w.shape[1] * data_size, w.shape[2] * model_size) for w in (w_fc1, w_fc2)]
        new_w1 = weight_step(w_fc1, back1, *full[0])
        new_w2 = weight_step(w_fc2, back2, *full[1])
        return new_w1, new_m1, new_w2, new_m2

    return jax.shard_map(local_step, mesh=mesh, in_specs=(block_spec,) * 6, out_specs=(block_spec,) * 4, check_vma=False)
```

time: 1340 us -> 513 us (0.38)
  matrix products: 709 us -> 0 us
  Pallas kernels: 0 us -> 467 us
  blocking collectives: 225 us -> 0 us
  waiting for transfers between devices: 165 us -> 0 us
  other arithmetic: 118 us -> 29 us
  local copies, waits for them, and re-layouts: 90.3 us -> 14.2 us
  starting transfers between devices: 18.1 us -> 0 us
  between operations: 14.3 us -> 0.67 us
    dot_general x22 -> x0, matrix products: 709 us -> none  [the longest x10 382 us: newton_schulz(): jnp.einsum('emk,ekn->emn', x_mat, poly_mat, preferred_element_type=jnp.fl...]
    pallas_call x0 -> x3, Pallas kernels: none -> 467 us  [the longest x1 413 us: exchange(): pl.pallas_call(exchange_kernel, in_specs=[any_spec] * 4, out_specs=[any_s...]
    psum x1 -> x0, blocking collectives: 150 us -> none  [update_stack(): lax.psum(jnp.sum(new_mom * new_mom, axis=(1, 2)), ('data', 'model'))]
    all_to_all x3 -> x0, waiting for transfers between devices: 103 us -> none  [the longest x2 103 us: update_stack(): x_back = lax.all_to_all(x_cols, 'data', 1, 0, tiled=True)]
    all_to_all x1 -> x0, blocking collectives: 75 us -> none  [update_stack(): lax.all_to_all(new_mom.astype(jnp.bfloat16), 'data', 0, 1, tiled=True)]
    all_gather x2 -> x0, waiting for transfers between devices: 62.5 us -> none  [update_stack(): mom_whole = lax.all_gather(row_whole, 'model', axis=2, tiled=True)]
    convert_element_type x4 -> x0, other arithmetic: 42.1 us -> none  [the longest x2 23.9 us: newton_schulz(): (NS_COEF_A * x_mat.astype(jnp.float32) + update_term).astype(jnp.bfloat16)]
    dynamic_slice x2 -> x0, local copies, waits for them, and re-layouts: 38.1 us -> none  [update_stack(): lax.dynamic_slice_in_dim(x_mat, lax.axis_index('model') * cols_loc, cols_...]
  transfers between devices with their start and end apart: 5 -> 0, of which waited for: 2 -> 0; matrix products, arithmetic and copies ran while one was open for 63% -> 0% of each run, Pallas kernels for 0% -> 0%
where the time goes in v1:
time: 513 us; the launch traced here: 511 us
  Pallas kernels  467 us (91%)
  other arithmetic  29 us (6%)
  local copies, waits for them, and re-layouts  14.2 us (3%)
    pallas_call x1, Pallas kernels, exchange(): pl.pallas_call(exchange_kernel, in_specs=[any_spec] * 4, out_specs=[any_s...  413 us
    pallas_call x2, Pallas kernels, momentum_step(): pl.pallas_call(momentum_kernel, grid=(experts,), in_specs=[block, block],...  53.8 us
    sub x2, other arithmetic, weight_step(): w_loc - LEARN_RATE * (x_back.astype(jnp.float32) * step_scale + DECAY * w...  29 us
    unnamed x14, local copies, waits for them, and re-layouts  14.2 us

profile of v1, /device:TPU:0, one launch (start us, length us, event | category | flops | bytes accessed | tf_op | source)
XLA Modules:
  0.0 511.1 jit_solution(16679177845932435076)
XLA Ops:
  0.6 0.0 copy-start
  0.6 2.8 copy-done
  3.4 21.2 %momentum.3 = (f32[32,384,256]{2,1,0:T(8,128)}, bf16[32,384,256]{2,1,0:T(8,128)(2,1)S(1)}, f32[8,4,8,128]{3,2,1,0:T(8,128)S(1)}) custom-call(f32[32,384,256]{2,1,0:T(8,128)} %m_ref.3, bf16[32,384,256]{2,1,0:T(8,128)(2,1)S(1)} %copy-done), custom_call_target="tpu_custom_call" | custom-call | tf_op jit(solution)/shard_map/momentum/pallas_call | solution.py:41
  24.7 0.0 copy-start.2
  24.7 2.7 copy-done.2
  27.4 0.0 copy-start.3
  27.4 0.7 copy-done.3
  28.0 32.6 %momentum.2 = (f32[32,384,512]{2,1,0:T(8,128)}, bf16[32,384,512]{2,1,0:T(8,128)(2,1)S(1)}, f32[8,4,8,128]{3,2,1,0:T(8,128)S(1)}) custom-call(f32[32,384,512]{2,1,0:T(8,128)} %m_ref.2, bf16[32,384,512]{2,1,0:T(8,128)(2,1)} %g_ref.2), custom_call_target="tpu_custom_call" | custom-call | tf_op jit(solution)/shard_map/momentum/pallas_call | solution.py:41
  60.6 0.0 copy-start.1
  60.6 4.8 copy-done.1
  65.4 0.0 copy-start.4
  65.4 0.7 copy-done.4
  66.1 413.4 %exchange.1 = (bf16[32,384,512]{2,1,0:T(8,128)(2,1)}, bf16[32,384,256]{2,1,0:T(8,128)(2,1)}) custom-call(bf16[32,384,512]{2,1,0:T(8,128)(2,1)} %copy-done.1, bf16[32,384,256]{2,1,0:T(8,128)(2,1)} %copy-done.2, f32[8,4,8,128]{3,2,1,0:T(8,128)} %copy-done.4, f32[8,4,8,128]{3,2,1,0:T(8,128)} %copy-done.3), custom_call_target="tpu_custom_call" | custom-call | flops 209379655680 | bytes 37748736 | tf_op jit(solution)/shard_map/exchange/pallas_call | solution.py:177
  479.4 0.0 copy-start.5
  479.5 0.0 copy-start.6
  479.5 23.2 %multiply_subtract_fusion = f32[32,384,512]{2,1,0:T(8,128)} fusion(f32[32,384,512]{2,1,0:T(8,128)} %param.6, bf16[32,384,512]{2,1,0:T(8,128)(2,1)} %get-tuple-element.16), kind=kLoop, calls=%fused_computation | loop fusion | flops 37748736 | bytes 62914560 | tf_op jit(solution)/shard_map/sub | solution.py:202
  502.7 0.6 copy-done.5
  503.3 2.1 copy-done.6
  505.4 5.7 %multiply_subtract_fusion.1 = f32[32,384,256]{2,1,0:T(8,128)} fusion(f32[32,384,256]{2,1,0:T(8,128)S(1)} %copy-done.5, bf16[32,384,256]{2,1,0:T(8,128)(2,1)S(1)} %copy-done.6), kind=kLoop, calls=%fused_computation.1 | loop fusion | flops 18874368 | bytes 31457280 | tf_op jit(solution)/shard_map/sub | solution.py:202
Async XLA Ops:
  0.6 2.8 copy-start
  24.7 2.7 copy-start.2
  27.4 0.7 copy-start.3
  60.6 4.8 copy-start.1
  65.4 0.7 copy-start.4
  479.4 23.9 %copy-start.5 = (f32[32,384,256]{2,1,0:T(8,128)S(1)}, f32[32,384,256]{2,1,0:T(8,128)}, u32[]{:S(2)}) copy-start(f32[32,384,256]{2,1,0:T(8,128)} %param.9) | copy-start | bytes 37748740
  479.5 25.9 %copy-start.6 = (bf16[32,384,256]{2,1,0:T(8,128)(2,1)S(1)}, bf16[32,384,256]{2,1,0:T(8,128)(2,1)}, u32[]{:S(2)}) copy-start(bf16[32,384,256]{2,1,0:T(8,128)(2,1)} %get-tuple-element.18) | copy-start | bytes 18874372

commit v2 on v1

v2 whole, which is shorter than its diff:
```python
import functools
import math
import jax
import jax.numpy as jnp
from jax import lax
from jax.experimental import pallas as pl
from jax.experimental.pallas import tpu as pltpu
from jax.sharding import PartitionSpec as P

NS_STEPS = 5
NS_COEF_A = 3.4445
NS_COEF_B = -4.7750
NS_COEF_C = 2.0315
MOMENTUM = 0.95
LEARN_RATE = 0.04
DECAY = 0.2
NORM_EPS = 1e-7

MESH_ID = pl.DeviceIdType.MESH
GRAM_BLOCK = 256
ROW_BLOCK = 512


def iterate(x_ref, gram_ref, poly_ref):
    rows, cols = x_ref.shape
    gram_block = min(GRAM_BLOCK, cols)
    row_block = min(ROW_BLOCK, rows)

    @pl.loop(0, NS_STEPS)
    def ns_step(_):
        @pl.loop(0, cols // gram_block)
        def gram(i):
            span = pl.ds(pl.multiple_of(i * gram_block, gram_block), gram_block)
            part = lax.dot_general(x_ref[:, span], x_ref[...], (((0,), (0,)), ((), ())), preferred_element_type=jnp.float32)
            gram_ref[span, :] = part.astype(jnp.bfloat16)

        @pl.loop(0, cols // gram_block)
        def poly(i):
            span = pl.ds(pl.multiple_of(i * gram_block, gram_block), gram_block)
            gram_rows = gram_ref[span, :]
            gram_sq = jnp.dot(gram_rows, gram_ref[...], preferred_element_type=jnp.float32)
            poly_ref[span, :] = (NS_COEF_B * gram_rows.astype(jnp.float32) + NS_COEF_C * gram_sq).astype(jnp.bfloat16)

        @pl.loop(0, rows // row_block)
        def update(i):
            span = pl.ds(pl.multiple_of(i * row_block, row_block), row_block)
            x_rows = x_ref[span, :]
            term = jnp.dot(x_rows, poly_ref[...], preferred_element_type=jnp.float32)
            x_ref[span, :] = (NS_COEF_A * x_rows.astype(jnp.float32) + term).astype(jnp.bfloat16)


def momentum_block(m_ref, g_ref, slot, low_ref, index, sq_ref, owner, k):
    new_mom = MOMENTUM * m_ref[slot] + g_ref[slot].astype(jnp.float32)
    low_ref[index] = new_mom.astype(jnp.bfloat16)
    squares = new_mom * new_mom
    rows, cols = squares.shape
    part = jnp.sum(squares.reshape(rows // 8, 8, cols), axis=0)
    total = part[:, :128]
    for start in range(128, cols, 128):
        total = total + part[:, start:start + 128]
    sq_ref[owner, k] = total


def exchange_kernel(m1, g1, m2, g2, back1, back2, last, low1, low2, x1, x2, sq1, sq2, sums1, sums2,
                    gram1, poly1, gram2, poly2, m_buf1, g_buf1, m_buf2, g_buf2,
                    fwd1, fwd2, got1, got2, ret1, ret2, done_sems, sq_send1, sq_send2, sq_got1, sq_got2,
                    m_sem1, g_sem1, m_sem2, g_sem2, last_sem):
    model = lax.axis_index('model')
    data = lax.axis_index('data')
    chip, core = data // 2, data % 2
    me = model * 4 + data
    owners = 8
    experts = m1.shape[0]
    rounds = experts // owners
    slots = m_buf1.shape[0]

    offsets = [(1, 0, 0), (0, 1, 0), (1, 0, 1), (0, 1, 1), (1, 1, 0), (1, 1, 1), (0, 0, 1)]
    others = [((model + dm) % 2, ((chip + dx) % 2) * 2 + (core + dc) % 2) for dm, dx, dc in offsets]

    def loads(m, g, m_buf, g_buf, m_sem, g_sem, index):
        slot = index % slots
        return (pltpu.make_async_copy(m.at[index], m_buf.at[slot], m_sem.at[slot]),
                pltpu.make_async_copy(g.at[index], g_buf.at[slot], g_sem.at[slot]))

    stack1 = (m1, g1, m_buf1, g_buf1, m_sem1, g_sem1)
    stack2 = (m2, g2, m_buf2, g_buf2, m_sem2, g_sem2)
    for stack in (stack2, stack1):
        for index in range(slots):
            for load in loads(*stack, index):
                load.start()

    barrier = pltpu.get_barrier_semaphore()
    for peer_model, peer_data in others:
        pl.semaphore_signal(barrier, inc=1, device_id=(0, peer_model, peer_data), device_id_type=MESH_ID)
    pl.semaphore_wait(barrier, len(others))

    def window(x_ref, k, at_model, at_data):
        rows, cols = x_ref.shape[1] // 4, x_ref.shape[2] // 2
        return x_ref.at[k, pl.ds(pl.multiple_of(at_data * rows, rows), rows), pl.ds(pl.multiple_of(at_model * cols, cols), cols)]

    def momentum_round(k, stack, low_ref, sq_ref):
        @pl.loop(0, owners)
        def block(owner):
            index = k * owners + owner
            for load in loads(*stack, index):
                load.wait()
            momentum_block(stack[2], stack[3], index % slots, low_ref, index, sq_ref, owner, k)

            @pl.when(index + slots < experts)
            def prefetch():
                for load in loads(*stack, index + slots):
                    load.start()

    def send_round(k, low_ref, x_ref, fwd, got, sq_ref, sums_ref, sq_send, sq_got):
        for peer_model, peer_data in others:
            owner = peer_model * 4 + peer_data
            to_owner = dict(device_id=(0, peer_model, peer_data), device_id_type=MESH_ID)
            pltpu.make_async_remote_copy(sq_ref.at[owner, k], sums_ref.at[k, me], sq_send.at[k], sq_got.at[k], **to_owner).start()
            pltpu.make_async_remote_copy(low_ref.at[k * owners + owner], window(x_ref, k, model, data), fwd.at[k], got.at[k],
                                         **to_owner).start()
        pltpu.make_async_copy(sq_ref.at[me, k], sums_ref.at[k, me], sq_got.at[k]).start()
        pltpu.make_async_copy(low_ref.at[k * owners + me], window(x_ref, k, model, data), got.at[k]).start()

    def return_round(k, x_ref, dst, sems, t, columns):
        @pl.when(k < rounds - 1)
        def to_holders():
            for peer_model, peer_data in others:
                pltpu.make_async_remote_copy(window(x_ref, k, peer_model, peer_data), dst.at[k * owners + me],
                                             sems.at[k], done_sems.at[t],
                                             device_id=(0, peer_model, peer_data), device_id_type=MESH_ID).start()
            pltpu.make_async_copy(window(x_ref, k, model, data), dst.at[k * owners + me], done_sems.at[t]).start()

        @pl.when(k == rounds - 1)
        def to_last():
            for holder in range(owners):
                pltpu.make_async_copy(window(x_ref, k, holder // 4, holder % 4), last.at[holder, :, columns], last_sem.at[t]).start()

    def wait_bytes(ref, sem):
        pltpu.make_async_copy(ref, ref, sem).wait()

    def orthogonalize(k, x_ref, got, sums_ref, sq_got, gram_ref, poly_ref):
        wait_bytes(sums_ref.at[k], sq_got.at[k])
        wait_bytes(x_ref.at[k], got.at[k])
        norm = jnp.sqrt(jnp.sum(sums_ref[k])) + NORM_EPS
        rows = x_ref.shape[1]

        @pl.loop(0, rows // 256)
        def normalize(i):
            span = pl.ds(pl.multiple_of(i * 256, 256), 256)
            x_ref[k, span, :] = (x_ref[k, span, :].astype(jnp.float32) / norm).astype(jnp.bfloat16)

        iterate(x_ref.at[k], gram_ref, poly_ref)

    @pl.loop(0, rounds)
    def forward(k):
        momentum_round(k, stack2, low2, sq2)
        send_round(k, low2, x2, fwd2, got2, sq2, sums2, sq_send2, sq_got2)
        momentum_round(k, stack1, low1, sq1)
        send_round(k, low1, x1, fwd1, got1, sq1, sums1, sq_send1, sq_got1)

    cols1, cols2 = low1.shape[2], low2.shape[2]

    @pl.loop(0, rounds)
    def work(k):
        orthogonalize(k, x2, got2, sums2, sq_got2, gram2, poly2)
        return_round(k, x2, back2, ret2, 0, pl.ds(cols1, cols2))
        orthogonalize(k, x1, got1, sums1, sq_got1, gram1, poly1)
        return_round(k, x1, back1, ret1, 1, pl.ds(0, cols1))

    count = len(others)

    @pl.loop(0, rounds)
    def finish(k):
        for low, sq, fwd, ret, sq_send in ((low2, sq2, fwd2, ret2, sq_send2), (low1, sq1, fwd1, ret1, sq_send1)):
            wait_bytes(sq.at[pl.ds(0, count), 0], sq_send.at[k])
            wait_bytes(low.at[pl.ds(0, count)], fwd.at[k])

            @pl.when(k < rounds - 1)
            def returned():
                wait_bytes(low.at[pl.ds(0, count)], ret.at[k])

    wait_bytes(back2, done_sems.at[0])
    wait_bytes(back1, done_sems.at[1])
    wait_bytes(last.at[:, :, pl.ds(cols1, cols2)], last_sem.at[0])
    wait_bytes(last.at[:, :, pl.ds(0, cols1)], last_sem.at[1])


def exchange(m1, g1, m2, g2, owners):
    experts, rows, cols1 = m1.shape
    cols2 = m2.shape[2]
    rounds = experts // owners
    slots = 4
    any_spec = pl.BlockSpec(memory_space=pl.ANY)
    flops = 2 * rounds * NS_STEPS * sum(2 * 4 * rows * c * c + c ** 3 for c in (2 * cols1, 2 * cols2))
    low = jnp.bfloat16
    dma = pltpu.SemaphoreType.DMA
    held = [jax.ShapeDtypeStruct((experts - owners, rows, c), low) for c in (cols1, cols2)]
    return pl.pallas_call(
        exchange_kernel,
        in_specs=[any_spec] * 4,
        out_specs=[any_spec] * 3,
        out_shape=held + [jax.ShapeDtypeStruct((owners, rows, cols1 + cols2), low)],
        scratch_shapes=[
            pltpu.VMEM((experts, rows, cols1), low),
            pltpu.VMEM((experts, rows, cols2), low),
            pltpu.VMEM((rounds, 4 * rows, 2 * cols1), low),
            pltpu.VMEM((rounds, 4 * rows, 2 * cols2), low),
            pltpu.VMEM((owners, rounds, 8, 128), jnp.float32),
            pltpu.VMEM((owners, rounds, 8, 128), jnp.float32),
            pltpu.VMEM((rounds, owners, 8, 128), jnp.float32),
            pltpu.VMEM((rounds, owners, 8, 128), jnp.float32),
            pltpu.VMEM((2 * cols1, 2 * cols1), low),
            pltpu.VMEM((2 * cols1, 2 * cols1), low),
            pltpu.VMEM((2 * cols2, 2 * cols2), low),
            pltpu.VMEM((2 * cols2, 2 * cols2), low),
            pltpu.VMEM((slots, rows, cols1), jnp.float32),
            pltpu.VMEM((slots, rows, cols1), low),
            pltpu.VMEM((slots, rows, cols2), jnp.float32),
            pltpu.VMEM((slots, rows, cols2), low),
        ] + [dma((rounds,))] * 6 + [dma((2,))] + [dma((rounds,))] * 4 + [dma((slots,))] * 4 + [dma((2,))],
        compiler_params=pltpu.CompilerParams(collective_id=0, has_side_effects=True, vmem_limit_bytes=60 * 2 ** 20),
        cost_estimate=pl.CostEstimate(flops=flops, bytes_accessed=10 * (m1.size + m2.size), transcendentals=0),
        name='exchange',
    )(m1, g1, m2, g2)


STEP = 4


def call_plain(kernel, name, steps, in_specs, out_specs, out_shape, args, aliases, traffic):
    return pl.pallas_call(
        kernel, grid=(steps,), in_specs=in_specs, out_specs=out_specs, out_shape=out_shape, input_output_aliases=aliases,
        compiler_params=pltpu.CompilerParams(dimension_semantics=('arbitrary',), vmem_limit_bytes=60 * 2 ** 20),
        cost_estimate=pl.CostEstimate(flops=traffic, bytes_accessed=traffic, transcendentals=0),
        name=name,
    )(*args)


def momentum_kernel(m1_ref, g1_ref, m2_ref, g2_ref, after_ref, new_m1_ref, new_m2_ref):
    new_m1_ref[...] = MOMENTUM * m1_ref[...] + g1_ref[...].astype(jnp.float32)
    new_m2_ref[...] = MOMENTUM * m2_ref[...] + g2_ref[...].astype(jnp.float32)


def momentum_step(m1, g1, m2, g2, after):
    blocks = [pl.BlockSpec((STEP,) + m.shape[1:], lambda i: (i, 0, 0)) for m in (m1, m2)]
    return call_plain(momentum_kernel, 'momentum', m1.shape[0] // STEP,
                      [blocks[0], blocks[0], blocks[1], blocks[1], pl.BlockSpec(memory_space=pl.ANY)], blocks,
                      [jax.ShapeDtypeStruct(m.shape, jnp.float32) for m in (m1, m2)],
                      (m1, g1, m2, g2, after), {}, 10 * (m1.size + m2.size))


def weight_kernel(scales, w1_ref, w2_ref, x1_ref, x2_ref, *refs):
    for scale, w_ref, x_ref, out_ref in zip(scales, (w1_ref, w2_ref), (x1_ref, x2_ref), refs[-2:]):
        w_old = w_ref[...]
        out_ref[...] = w_old - LEARN_RATE * (x_ref[...].astype(jnp.float32) * scale + DECAY * w_old)


def weight_step(w1, w2, x1, x2, scales, first, count, x_columns, into):
    start = first // STEP
    w_specs = [pl.BlockSpec((STEP,) + w.shape[1:], lambda i: (start + i, 0, 0)) for w in (w1, w2)]
    x_specs = [pl.BlockSpec((STEP,) + w.shape[1:], lambda i, c=c: (i, 0, c)) for w, c in zip((w1, w2), x_columns)]
    return call_plain(functools.partial(weight_kernel, scales), 'weights', count // STEP,
                      w_specs + x_specs + [pl.BlockSpec(memory_space=pl.ANY)] * len(into), w_specs,
                      [jax.ShapeDtypeStruct(w.shape, w.dtype) for w in (w1, w2)],
                      (w1, w2, x1, x2, *into), {4 + i: i for i in range(len(into))},
                      10 * count * (w1.size + w2.size) // w1.shape[0])


def solution(mesh):
    data_size = mesh.shape['data']
    model_size = mesh.shape['model']
    owners = data_size * model_size
    block_spec = P('stage', 'data', 'model')

    def local_step(w_fc1, m_fc1, g_fc1, w_fc2, m_fc2, g_fc2):
        experts = w_fc1.shape[0]
        head = experts - owners
        scales = [0.2 * math.sqrt(max(w.shape[1] * data_size, w.shape[2] * model_size)) for w in (w_fc1, w_fc2)]
        back1, back2, last = exchange(m_fc1, g_fc1, m_fc2, g_fc2, owners)
        last = lax.all_to_all(last, ('model', 'data'), 0, 0, tiled=True)
        new_m1, new_m2 = momentum_step(m_fc1, g_fc1, m_fc2, g_fc2, back1)
        part = weight_step(w_fc1, w_fc2, back1, back2, scales, 0, head, (0, 0), ())
        tail_column = w_fc1.shape[2] // w_fc2.shape[2]
        new_w1, new_w2 = weight_step(w_fc1, w_fc2, last, last, scales, head, owners, (0, tail_column), part)
        return new_w1, new_m1, new_w2, new_m2

    return jax.shard_map(local_step, mesh=mesh, in_specs=(block_spec,) * 6, out_specs=(block_spec,) * 4, check_vma=False)
```

time: 513 us -> 434 us (0.85)
  Pallas kernels: 467 us -> 429 us
  other arithmetic: 29 us -> 0 us
  local copies, waits for them, and re-layouts: 14.2 us -> 0 us
    pallas_call x1, Pallas kernels: 413 us -> 366 us  [exchange(): pl.pallas_call(exchange_kernel, in_specs=[any_spec] * 4, out_specs=[any_s...]
    sub x2 -> x0, other arithmetic: 29 us -> none  [weight_step(): w_loc - LEARN_RATE * (x_back.astype(jnp.float32) * step_scale + DECAY * w...]
    unnamed x14 -> x0, local copies, waits for them, and re-layouts: 14.2 us -> none
    pallas_call x2 -> x3, Pallas kernels: 53.8 us -> 62.8 us  [call_plain(): pl.pallas_call(kernel, grid=(steps,), in_specs=in_specs, out_specs=out_sp...]
  transfers between devices with their start and end apart: 0 -> 1, of which waited for: 0 -> 1; matrix products, arithmetic and copies ran while one was open for 0% -> 0% of each run, Pallas kernels for 0% -> 12%
where the time goes in v2:
time: 434 us; the launch traced here: 433 us
  Pallas kernels  429 us (99%)
    pallas_call x1, Pallas kernels, exchange(): pl.pallas_call(exchange_kernel, in_specs=[any_spec] * 4, out_specs=[any_s...  366 us
    pallas_call x3, Pallas kernels, call_plain(): pl.pallas_call(kernel, grid=(steps,), in_specs=in_specs, out_specs=out_sp...  62.8 us
  transfers between devices with their start and end apart: 1, of which 1 were waited for; matrix products, arithmetic and copies ran while one was open for 0% of the time, Pallas kernels for 12%

profile of v2, /device:TPU:0, one launch (start us, length us, event | category | flops | bytes accessed | tf_op | source)
XLA Modules:
  0.0 433.3 jit_solution(8982138203580062259)
XLA Ops:
  0.6 365.9 %exchange.1 = (bf16[24,384,512]{2,1,0:T(8,128)(2,1)}, bf16[24,384,256]{2,1,0:T(8,128)(2,1)}, bf16[8,384,768]{2,1,0:T(8,128)(2,1)}) custom-call(f32[32,384,512]{2,1,0:T(8,128)} %m1_ref.1, bf16[32,384,512]{2,1,0:T(8,128)(2,1)} %g1_ref.1, f32[32,384,256]{2,1,0:T(8,128)} %m2_ref.1, bf16[32,384,256]{2,1,0:T(8,128)(2,1)} %g2_ref.1), custom_call_target="tpu_custom_call" | custom-call | flops 209379655680 | bytes 94371840 | tf_op jit(solution)/shard_map/exchange/pallas_call | solution.py:198
  366.6 3.3 all-to-all-start
  369.9 22.8 %weights.2 = (f32[32,384,512]{2,1,0:T(8,128)}, f32[32,384,256]{2,1,0:T(8,128)}) custom-call(f32[32,384,512]{2,1,0:T(8,128)} %w1_ref.3, f32[32,384,256]{2,1,0:T(8,128)} %w2_ref.3, bf16[24,384,512]{2,1,0:T(8,128)(2,1)} %get-tuple-element.14.x1_ref.after_ref, bf16[24,384,256]{2,1,0:T(8,128)(2,1)} %get-tuple-element.15.x2_ref), custom_call_target="tpu_custom_call" | custom-call | flops 70778880 | bytes 70778880 | tf_op jit(solution)/shard_map/weights/pallas_call | solution.py:231
  392.8 31.2 %momentum.1 = (f32[32,384,512]{2,1,0:T(8,128)}, f32[32,384,256]{2,1,0:T(8,128)}) custom-call(f32[32,384,512]{2,1,0:T(8,128)} %m1_ref.1, bf16[32,384,512]{2,1,0:T(8,128)(2,1)} %g1_ref.1, f32[32,384,256]{2,1,0:T(8,128)} %m2_ref.1, bf16[32,384,256]{2,1,0:T(8,128)(2,1)} %g2_ref.1, bf16[24,384,512]{2,1,0:T(8,128)(2,1)} %get-tuple-element.14.x1_ref.after_ref), custom_call_target="tpu_custom_call" | custom-call | flops 94371840 | bytes 94371840 | tf_op jit(solution)/shard_map/momentum/pallas_call | solution.py:231
  424.0 0.6 all-to-all-done.x1_ref.x2_ref
  424.5 8.7 %weights.3 = (f32[32,384,512]{2,1,0:T(8,128)}, f32[32,384,256]{2,1,0:T(8,128)}) custom-call(f32[32,384,512]{2,1,0:T(8,128)} %w1_ref.3, f32[32,384,256]{2,1,0:T(8,128)} %w2_ref.3, bf16[8,384,768]{2,1,0:T(8,128)(2,1)} %all-to-all-done.x1_ref.x2_ref, bf16[8,384,768]{2,1,0:T(8,128)(2,1)} %all-to-all-done.x1_ref.x2_ref, ...), custom_call_target="tpu_custom_call", output_to_operand_aliasing={{0}: (4, {}), {1}: (5, {})} | custom-call | flops 23592960 | bytes 23592960 | tf_op jit(solution)/shard_map/weights/pallas_call | solution.py:231
Async XLA Ops:
  366.6 58.0 %all-to-all-start = ((bf16[8,384,768]{2,1,0:T(8,128)(2,1)}), bf16[8,384,768]{2,1,0:T(8,128)(2,1)}, u32[]{:S(2)}, u32[]{:S(2)}) async-start(bf16[8,384,768]{2,1,0:T(8,128)(2,1)} %get-tuple-element.13), calls=%async_computation | async-start | bytes 9437184 | tf_op jit(solution)/shard_map/all_to_all | solution.py:280

commit v3 on v2

v3 whole, which is shorter than its diff:
```python
import functools
import math
import jax
import jax.numpy as jnp
from jax import lax
from jax.experimental import pallas as pl
from jax.experimental.pallas import tpu as pltpu
from jax.sharding import PartitionSpec as P

NS_STEPS = 5
NS_COEF_A = 3.4445
NS_COEF_B = -4.7750
NS_COEF_C = 2.0315
MOMENTUM = 0.95
LEARN_RATE = 0.04
DECAY = 0.2
NORM_EPS = 1e-7

MESH_ID = pl.DeviceIdType.MESH
GRAM_BLOCK = 256
ROW_BLOCK = 512


def iterate(x_ref, gram_ref, poly_ref):
    rows, cols = x_ref.shape
    gram_block = min(GRAM_BLOCK, cols)
    row_block = min(ROW_BLOCK, rows)

    @pl.loop(0, NS_STEPS)
    def ns_step(_):
        @pl.loop(0, cols // gram_block)
        def gram(i):
            span = pl.ds(pl.multiple_of(i * gram_block, gram_block), gram_block)
            part = lax.dot_general(x_ref[:, span], x_ref[...], (((0,), (0,)), ((), ())), preferred_element_type=jnp.float32)
            gram_ref[span, :] = part.astype(jnp.bfloat16)

        @pl.loop(0, cols // gram_block)
        def poly(i):
            span = pl.ds(pl.multiple_of(i * gram_block, gram_block), gram_block)
            gram_rows = gram_ref[span, :]
            gram_sq = jnp.dot(gram_rows, gram_ref[...], preferred_element_type=jnp.float32)
            poly_ref[span, :] = (NS_COEF_B * gram_rows.astype(jnp.float32) + NS_COEF_C * gram_sq).astype(jnp.bfloat16)

        @pl.loop(0, rows // row_block)
        def update(i):
            span = pl.ds(pl.multiple_of(i * row_block, row_block), row_block)
            x_rows = x_ref[span, :]
            term = jnp.dot(x_rows, poly_ref[...], preferred_element_type=jnp.float32)
            x_ref[span, :] = (NS_COEF_A * x_rows.astype(jnp.float32) + term).astype(jnp.bfloat16)


def momentum_block(m_ref, g_ref, slot, low_ref, index, sq_ref, owner, k):
    new_mom = MOMENTUM * m_ref[slot] + g_ref[slot].astype(jnp.float32)
    m_ref[slot] = new_mom
    low_ref[index] = new_mom.astype(jnp.bfloat16)
    squares = new_mom * new_mom
    rows, cols = squares.shape
    part = jnp.sum(squares.reshape(rows // 8, 8, cols), axis=0)
    total = part[:, :128]
    for start in range(128, cols, 128):
        total = total + part[:, start:start + 128]
    sq_ref[owner, k] = total


AHEAD = 3


def exchange_kernel(m1, g1, m2, g2, new_m1, new_m2, back1, back2, late, low1, low2, x1, x2, sq1, sq2, sums1, sums2,
                    gram1, poly1, gram2, poly2, m_buf1, g_buf1, m_buf2, g_buf2,
                    fwd1, fwd2, got1, got2, ret1, ret2, done_sems, sq_send1, sq_send2, sq_got1, sq_got2,
                    m_sem1, g_sem1, m_sem2, g_sem2, out_sem1, out_sem2, late_sem):
    model = lax.axis_index('model')
    data = lax.axis_index('data')
    chip, core = data // 2, data % 2
    me = model * 4 + data
    owners = 8
    experts = m1.shape[0]
    rounds = experts // owners
    slots = m_buf1.shape[0]
    early1, early2 = back1.shape[0] // owners, back2.shape[0] // owners

    def peer(turn):
        code = owners - 1 - turn
        return (model + code // 4) % 2, ((chip + code // 2 % 2) % 2) * 2 + (core + code % 2) % 2

    def at(place):
        return dict(device_id=(0, place[0], place[1]), device_id_type=MESH_ID)

    def expert(step):
        peer_model, peer_data = peer(step % owners)
        return step // owners * owners + peer_model * 4 + peer_data

    stack1 = (m1, g1, m_buf1, g_buf1, m_sem1, g_sem1)
    stack2 = (m2, g2, m_buf2, g_buf2, m_sem2, g_sem2)

    def loads(stack, step):
        m, g, m_buf, g_buf, m_sem, g_sem = stack
        slot, index = step % slots, expert(step)
        return (pltpu.make_async_copy(m.at[index], m_buf.at[slot], m_sem.at[slot]),
                pltpu.make_async_copy(g.at[index], g_buf.at[slot], g_sem.at[slot]))

    def store(stack, new_m, out_sem, step):
        slot = step % slots
        return pltpu.make_async_copy(stack[2].at[slot], new_m.at[expert(step)], out_sem.at[slot])

    for stack in (stack2, stack1):
        for step in range(AHEAD):
            for load in loads(stack, step):
                load.start()

    barrier = pltpu.get_barrier_semaphore()
    for turn in range(owners - 1):
        pl.semaphore_signal(barrier, inc=1, **at(peer(turn)))
    pl.semaphore_wait(barrier, owners - 1)

    def window(x_ref, k, at_model, at_data):
        rows, cols = x_ref.shape[1] // 4, x_ref.shape[2] // 2
        return x_ref.at[k, pl.ds(pl.multiple_of(at_data * rows, rows), rows), pl.ds(pl.multiple_of(at_model * cols, cols), cols)]

    def forward_round(k, stack, new_m, out_sem, low_ref, x_ref, fwd, got, sq_ref, sums_ref, sq_send, sq_got):
        def send(turn):
            place = peer(turn)
            owner = place[0] * 4 + place[1]
            pltpu.make_async_remote_copy(sq_ref.at[owner, k], sums_ref.at[k, me], sq_send.at[k], sq_got.at[k], **at(place)).start()
            pltpu.make_async_remote_copy(low_ref.at[k * owners + owner], window(x_ref, k, model, data), fwd.at[k], got.at[k],
                                         **at(place)).start()

        @pl.loop(0, owners)
        def block(turn):
            step = k * owners + turn
            index = expert(step)
            for load in loads(stack, step):
                load.wait()
            momentum_block(stack[2], stack[3], step % slots, low_ref, index, sq_ref, index - k * owners, k)
            store(stack, new_m, out_sem, step).start()

            @pl.when(turn > 0)
            def send_before():
                send(turn - 1)

            @pl.when(step >= slots - AHEAD)
            def stored():
                store(stack, new_m, out_sem, step + AHEAD - slots).wait()

            @pl.when(step + AHEAD < experts)
            def prefetch():
                for load in loads(stack, step + AHEAD):
                    load.start()

        pltpu.make_async_copy(sq_ref.at[me, k], sums_ref.at[k, me], sq_got.at[k]).start()
        pltpu.make_async_copy(low_ref.at[k * owners + me], window(x_ref, k, model, data), got.at[k]).start()

    def return_round(k, x_ref, dst, sems, t):
        for turn in range(owners - 1):
            place = peer(turn)
            pltpu.make_async_remote_copy(window(x_ref, k, *place), dst.at[k * owners + me], sems.at[k], done_sems.at[t],
                                         **at(place)).start()
        pltpu.make_async_copy(window(x_ref, k, model, data), dst.at[k * owners + me], done_sems.at[t]).start()

    def keep_round(k, x_ref, columns, sem):
        for holder in range(owners):
            pltpu.make_async_copy(window(x_ref, k, holder // 4, holder % 4), late.at[holder, :, columns], sem).start()

    def wait_bytes(ref, sem):
        pltpu.make_async_copy(ref, ref, sem).wait()

    def orthogonalize(k, x_ref, got, sums_ref, sq_got, gram_ref, poly_ref):
        wait_bytes(sums_ref.at[k], sq_got.at[k])
        wait_bytes(x_ref.at[k], got.at[k])
        norm = jnp.sqrt(jnp.sum(sums_ref[k])) + NORM_EPS
        rows = x_ref.shape[1]

        @pl.loop(0, rows // 256)
        def normalize(i):
            span = pl.ds(pl.multiple_of(i * 256, 256), 256)
            x_ref[k, span, :] = (x_ref[k, span, :].astype(jnp.float32) / norm).astype(jnp.bfloat16)

        iterate(x_ref.at[k], gram_ref, poly_ref)

    @pl.loop(0, rounds)
    def forward(k):
        forward_round(k, stack2, new_m2, out_sem2, low2, x2, fwd2, got2, sq2, sums2, sq_send2, sq_got2)
        forward_round(k, stack1, new_m1, out_sem1, low1, x1, fwd1, got1, sq1, sums1, sq_send1, sq_got1)

    cols1, cols2 = low1.shape[2], low2.shape[2]
    part1, part2 = pl.ds(0, cols1), pl.ds(cols1, cols2)

    @pl.loop(0, rounds)
    def work(k):
        orthogonalize(k, x2, got2, sums2, sq_got2, gram2, poly2)

        @pl.when(k < early2)
        def return2():
            return_round(k, x2, back2, ret2, 0)

        @pl.when(k == early2)
        def keep2():
            keep_round(k, x2, part2, late_sem.at[0])

        orthogonalize(k, x1, got1, sums1, sq_got1, gram1, poly1)

        @pl.when(k < early1)
        def return1():
            return_round(k, x1, back1, ret1, 1)

        @pl.when(k == early1)
        def keep1():
            keep_round(k, x1, part1, late_sem.at[1])

    count = owners - 1
    for stack, new_m, out_sem in ((stack2, new_m2, out_sem2), (stack1, new_m1, out_sem1)):
        for step in range(experts + AHEAD - slots, experts):
            store(stack, new_m, out_sem, step).wait()

    @pl.loop(0, rounds)
    def finish(k):
        for low, sq, fwd, ret, sq_send, early in ((low2, sq2, fwd2, ret2, sq_send2, early2), (low1, sq1, fwd1, ret1, sq_send1, early1)):
            wait_bytes(sq.at[pl.ds(0, count), 0], sq_send.at[k])
            wait_bytes(low.at[pl.ds(0, count)], fwd.at[k])

            @pl.when(k < early)
            def returned():
                wait_bytes(low.at[pl.ds(0, count)], ret.at[k])

    wait_bytes(back2, done_sems.at[0])
    wait_bytes(back1, done_sems.at[1])
    wait_bytes(late.at[:, :, part2], late_sem.at[0])
    wait_bytes(late.at[:, :, part1], late_sem.at[1])


def exchange(m1, g1, m2, g2, owners):
    experts, rows, cols1 = m1.shape
    cols2 = m2.shape[2]
    rounds = experts // owners
    slots = 2 * AHEAD
    any_spec = pl.BlockSpec(memory_space=pl.ANY)
    flops = 2 * rounds * NS_STEPS * sum(2 * 4 * rows * c * c + c ** 3 for c in (2 * cols1, 2 * cols2))
    low = jnp.bfloat16
    dma = pltpu.SemaphoreType.DMA
    results = [((experts, rows, cols1), jnp.float32), ((experts, rows, cols2), jnp.float32),
               ((experts - owners, rows, cols1), low), ((experts - owners, rows, cols2), low),
               ((owners, rows, cols1 + cols2), low)]
    return pl.pallas_call(
        exchange_kernel,
        in_specs=[any_spec] * 4,
        out_specs=[any_spec] * len(results),
        out_shape=[jax.ShapeDtypeStruct(*result) for result in results],
        scratch_shapes=[
            pltpu.VMEM((experts, rows, cols1), low),
            pltpu.VMEM((experts, rows, cols2), low),
            pltpu.VMEM((rounds, 4 * rows, 2 * cols1), low),
            pltpu.VMEM((rounds, 4 * rows, 2 * cols2), low),
            pltpu.VMEM((owners, rounds, 8, 128), jnp.float32),
            pltpu.VMEM((owners, rounds, 8, 128), jnp.float32),
            pltpu.VMEM((rounds, owners, 8, 128), jnp.float32),
            pltpu.VMEM((rounds, owners, 8, 128), jnp.float32),
            pltpu.VMEM((2 * cols1, 2 * cols1), low),
            pltpu.VMEM((2 * cols1, 2 * cols1), low),
            pltpu.VMEM((2 * cols2, 2 * cols2), low),
            pltpu.VMEM((2 * cols2, 2 * cols2), low),
            pltpu.VMEM((slots, rows, cols1), jnp.float32),
            pltpu.VMEM((slots, rows, cols1), low),
            pltpu.VMEM((slots, rows, cols2), jnp.float32),
            pltpu.VMEM((slots, rows, cols2), low),
        ] + [dma((rounds,))] * 6 + [dma((2,))] + [dma((rounds,))] * 4 + [dma((slots,))] * 6 + [dma((2,))],
        compiler_params=pltpu.CompilerParams(collective_id=0, has_side_effects=True, vmem_limit_bytes=62 * 2 ** 20),
        cost_estimate=pl.CostEstimate(flops=flops, bytes_accessed=14 * (m1.size + m2.size), transcendentals=0),
        name='exchange',
    )(m1, g1, m2, g2)


def call_plain(kernel, name, steps, in_specs, out_specs, out_shape, args, aliases, traffic):
    return pl.pallas_call(
        kernel, grid=(steps,), in_specs=in_specs, out_specs=out_specs, out_shape=out_shape, input_output_aliases=aliases,
        compiler_params=pltpu.CompilerParams(dimension_semantics=('arbitrary',), vmem_limit_bytes=60 * 2 ** 20),
        cost_estimate=pl.CostEstimate(flops=traffic, bytes_accessed=traffic, transcendentals=0),
        name=name,
    )(*args)


def weight_block(w_ref, x_ref, out_ref, scale):
    w_old = w_ref[...]
    out_ref[...] = w_old - LEARN_RATE * (x_ref[...].astype(jnp.float32) * scale + DECAY * w_old)


def early_kernel(scales, m1_ref, m2_ref, w1_ref, w2_ref, x1_ref, x2_ref, new_m1_ref, new_m2_ref, new_w1_ref, new_w2_ref):
    new_m1_ref[...] = m1_ref[...]
    new_m2_ref[...] = m2_ref[...]
    weight_block(w1_ref, x1_ref, new_w1_ref, scales[0])
    weight_block(w2_ref, x2_ref, new_w2_ref, scales[1])


def early_step(m1, m2, w1, w2, x1, x2, scales):
    experts, rows = m1.shape[:2]
    back = x1.shape[0]
    steps = 2 * (experts - back)

    def halves(array, count):
        return pl.BlockSpec((count * 2 // steps, rows // 2, array.shape[2]), lambda i: (i // 2, i % 2, 0))

    m_specs = [halves(m, experts) for m in (m1, m2)]
    w_specs = [halves(w, back) for w in (w1, w2)]
    outs = [jax.ShapeDtypeStruct(array.shape, array.dtype) for array in (m1, m2, w1, w2)]
    traffic = 8 * (m1.size + m2.size) + 10 * (x1.size + x2.size)
    return call_plain(functools.partial(early_kernel, scales), 'early', steps, m_specs + w_specs + w_specs, m_specs + w_specs,
                      outs, (m1, m2, w1, w2, x1, x2), {}, traffic)


def late_kernel(scales, w1_ref, w2_ref, x1_ref, x2_ref, into1_ref, into2_ref, new_w1_ref, new_w2_ref):
    weight_block(w1_ref, x1_ref, new_w1_ref, scales[0])
    weight_block(w2_ref, x2_ref, new_w2_ref, scales[1])


def late_step(w1, w2, late, into1, into2, scales):
    count = late.shape[0]
    first = w1.shape[0] - count
    column = w1.shape[2] // w2.shape[2]
    w_specs = [pl.BlockSpec((1,) + w.shape[1:], lambda i: (first + i, 0, 0)) for w in (w1, w2)]
    x_specs = [pl.BlockSpec((1,) + w.shape[1:], lambda i, c=c: (i, 0, c)) for w, c in ((w1, 0), (w2, column))]
    return call_plain(functools.partial(late_kernel, scales), 'late', count,
                      w_specs + x_specs + [pl.BlockSpec(memory_space=pl.ANY)] * 2, w_specs,
                      [jax.ShapeDtypeStruct(w.shape, w.dtype) for w in (w1, w2)],
                      (w1, w2, late, late, into1, into2), {4: 0, 5: 1}, 10 * late.size)


def solution(mesh):
    data_size = mesh.shape['data']
    model_size = mesh.shape['model']
    owners = data_size * model_size
    block_spec = P('stage', 'data', 'model')

    def local_step(w_fc1, m_fc1, g_fc1, w_fc2, m_fc2, g_fc2):
        scales = [0.2 * math.sqrt(max(w.shape[1] * data_size, w.shape[2] * model_size)) for w in (w_fc1, w_fc2)]
        new_m1, new_m2, back1, back2, late = exchange(m_fc1, g_fc1, m_fc2, g_fc2, owners)
        late = lax.all_to_all(late, ('model', 'data'), 0, 0, tiled=True)
        new_m1, new_m2, new_w1, new_w2 = early_step(new_m1, new_m2, w_fc1, w_fc2, back1, back2, scales)
        new_w1, new_w2 = late_step(w_fc1, w_fc2, late, new_w1, new_w2, scales)
        return new_w1, new_m1, new_w2, new_m2

    return jax.shard_map(local_step, mesh=mesh, in_specs=(block_spec,) * 6, out_specs=(block_spec,) * 4, check_vma=False)
```

time: 434 us -> 434 us (level)
  waiting for transfers between devices: 0.55 us -> 6.71 us
  Pallas kernels: 429 us -> 423 us
    all_to_all x1, waiting for transfers between devices: 0.55 us -> 6.71 us  [local_step(): late = lax.all_to_all(late, ('model', 'data'), 0, 0, tiled=True)]
    pallas_call x3 -> x2, Pallas kernels: 62.8 us -> 58.5 us  [call_plain(): pl.pallas_call(kernel, grid=(steps,), in_specs=in_specs, out_specs=out_sp...]
  transfers between devices with their start and end apart: 1 -> 1, of which waited for: 1 -> 1; matrix products, arithmetic and copies ran while one was open for 0% -> 0% of each run, Pallas kernels for 12% -> 11%
where the time goes in v3:
time: 434 us; the launch traced here: 433 us
  Pallas kernels  423 us (97%)
  waiting for transfers between devices  6.71 us (2%)
    pallas_call x1, Pallas kernels, exchange(): pl.pallas_call(exchange_kernel, in_specs=[any_spec] * 4, out_specs=[any_s...  364 us
    pallas_call x2, Pallas kernels, call_plain(): pl.pallas_call(kernel, grid=(steps,), in_specs=in_specs, out_specs=out_sp...  58.5 us
  transfers between devices with their start and end apart: 1, of which 1 were waited for; matrix products, arithmetic and copies ran while one was open for 0% of the time, Pallas kernels for 11%

profile of v3, /device:TPU:0, one launch (start us, length us, event | category | flops | bytes accessed | tf_op | source)
XLA Modules:
  0.0 433.4 jit_solution(17708668752234267983)
XLA Ops:
  0.6 364.2 %exchange.1 = (f32[32,384,512]{2,1,0:T(8,128)}, f32[32,384,256]{2,1,0:T(8,128)}, bf16[24,384,512]{2,1,0:T(8,128)(2,1)}, bf16[24,384,256]{2,1,0:T(8,128)(2,1)}, bf16[8,384,768]{2,1,0:T(8,128)(2,1)}) custom-call(f32[32,384,512]{2,1,0:T(8,128)} %m1.1, bf16[32,384,512]{2,1,0:T(8,128)(2,1)} %g1.1, f32[32,384,256]{2,1,0:T(8,128)} %m2.1, bf16[32,384,256]{2,1,0:T(8,128)(2,1)} %g2.1), custom_call_target="tpu_custom_call" | custom-call | flops 209379655680 | bytes 132120576 | tf_op jit(solution)/shard_map/exchange/pallas_call | solution.py:243
  364.9 3.4 all-to-all-start
  368.3 47.9 %early.1 = (f32[32,384,512]{2,1,0:T(8,128)}, f32[32,384,256]{2,1,0:T(8,128)}, f32[32,384,512]{2,1,0:T(8,128)}, f32[32,384,256]{2,1,0:T(8,128)}) custom-call(f32[32,384,512]{2,1,0:T(8,128)} %get-tuple-element.16.m1_ref, f32[32,384,256]{2,1,0:T(8,128)} %get-tuple-element.17.m2_ref, f32[32,384,512]{2,1,0:T(8,128)} %w1_ref.3, f32[32,384,256]{2,1,0:T(8,128)} %w2_ref.3, ...), custom_call_target="tpu_custom_call" | custom-call | flops 146276352 | bytes 146276352 | tf_op jit(solution)/shard_map/early/pallas_call | solution.py:273
  416.2 6.7 %all-to-all-done.x1_ref.x2_ref = bf16[8,384,768]{2,1,0:T(8,128)(2,1)} async-done(((bf16[8,384,768]{2,1,0:T(8,128)(2,1)}), bf16[8,384,768]{2,1,0:T(8,128)(2,1)}, u32[]{:S(2)}, u32[]{:S(2)}) %all-to-all-start) | async-done | bytes 4718624 | tf_op jit(solution)/shard_map/all_to_all | solution.py:335
  422.9 10.5 %late.1 = (f32[32,384,512]{2,1,0:T(8,128)}, f32[32,384,256]{2,1,0:T(8,128)}) custom-call(f32[32,384,512]{2,1,0:T(8,128)} %w1_ref.3, f32[32,384,256]{2,1,0:T(8,128)} %w2_ref.3, bf16[8,384,768]{2,1,0:T(8,128)(2,1)} %all-to-all-done.x1_ref.x2_ref, bf16[8,384,768]{2,1,0:T(8,128)(2,1)} %all-to-all-done.x1_ref.x2_ref, ...), custom_call_target="tpu_custom_call", output_to_operand_aliasing={{0}: (4, {}), {1}: (5, {})} | custom-call | flops 23592960 | bytes 23592960 | tf_op jit(solution)/shard_map/late/pallas_call | solution.py:273
Async XLA Ops:
  364.9 58.0 %all-to-all-start = ((bf16[8,384,768]{2,1,0:T(8,128)(2,1)}), bf16[8,384,768]{2,1,0:T(8,128)(2,1)}, u32[]{:S(2)}, u32[]{:S(2)}) async-start(bf16[8,384,768]{2,1,0:T(8,128)(2,1)} %get-tuple-element.15), calls=%async_computation | async-start | bytes 9437184 | tf_op jit(solution)/shard_map/all_to_all | solution.py:335
